TPU v7x, 32 devices: a 4x2x2 block of a 4x4x8 slice. The times are simulated.
32 devices in a mesh: dp: 4 (over y, z), tp: 8 (over x, core).
Axes of the slice: x: 4, y: 2, z: 2, core: 2. Of those that a mesh axis runs over, the one named last changes fastest.
The devices are a block of a 4x4x8 slice.
Arguments:
- hidden: bfloat16 [16384, 8192], P(('dp', 'tp')), parts along dimension 0
- norm_gain: float32 [8192], replicated
- w_query: bfloat16 [8192, 64, 128], P(None, 'tp')
- w_key: bfloat16 [8192, 64, 128], P(None, 'tp')
- w_value: bfloat16 [8192, 64, 128], P(None, 'tp')
Outputs:
- output 1: bfloat16 [16384, 64, 128], P('dp', 'tp'), parts along dimension 0
- output 2: bfloat16 [16384, 64, 128], P('dp', 'tp'), parts along dimension 0
- output 3: bfloat16 [16384, 64, 128], P('dp', 'tp'), parts along dimension 0
There are 4 independent parts. A program takes and returns all parts, laid end to end along the dimension named above; an argument that names none is the same for every part.
All inputs are finite; a program needn't handle non-finite values.
Results may differ from a plain program's by a relative error of at most 0.001.
Values are sent between devices in bfloat16 or wider.
A program may use at most 768 MiB of HBM per device.

v0:
```python
import jax
import jax.numpy as jnp
from jax import lax
from jax.sharding import PartitionSpec as P


def solution(mesh):
    def local_step(hidden_blk, norm_gain, wq_local, wk_local, wv_local):
        hidden_f32 = hidden_blk.astype(jnp.float32)
        mean_sq = jnp.mean(hidden_f32 * hidden_f32, axis=-1, keepdims=True)
        normed = (hidden_f32 * lax.rsqrt(mean_sq + 1e-6) * norm_gain).astype(jnp.bfloat16)
        gathered = lax.all_gather(normed, "tp", axis=0, tiled=True)
        q_out = jnp.einsum("td,dhk->thk", gathered, wq_local, preferred_element_type=jnp.float32).astype(jnp.bfloat16)
        k_out = jnp.einsum("td,dhk->thk", gathered, wk_local, preferred_element_type=jnp.float32).astype(jnp.bfloat16)
        v_out = jnp.einsum("td,dhk->thk", gathered, wv_local, preferred_element_type=jnp.float32).astype(jnp.bfloat16)
        return q_out, k_out, v_out

    row_spec = P(("dp", "tp"), None)
    head_spec = P(None, "tp", None)
    out_spec = P("dp", "tp", None)
    return jax.shard_map(local_step, mesh=mesh, in_specs=(row_spec, P(None), head_spec, head_spec, head_spec), out_specs=(out_spec, out_spec, out_spec), check_vma=False)
```

profile of v0, /device:TPU:81, one launch (start us, length us, event | category | flops | bytes accessed | tf_op | source)
XLA Modules:
  0.0 598.1 jit_solution(18003157086057673787)
XLA Ops:
  7.2 0.1 all-gather.2.cloned.1.call-start
  7.2 5.1 fusion.6
  12.4 10.0 %fusion.8 = bf16[512,8192]{1,0:T(8,128)(2,1)} fusion(bf16[512,8192]{1,0:T(8,128)(2,1)} %param.5, f32[8192]{0:T(1024)} %param.6, f32[512]{0:T(512)S(1)} %add_rsqrt_fusion), kind=kLoop, calls=%fused_computation.10 | loop fusion | flops 16777216 | bytes 16812032 | tf_op jit(solution)/shard_map/convert_element_type | solution.py:11
  22.4 0.1 all-gather.2.cloned.1.call-update
  22.4 298.9 %all-gather.2.cloned.1.call-done = bf16[4096,8192]{1,0:T(8,128)(2,1)} async-done(((bf16[512,8192]{1,0:T(8,128)(2,1)}), bf16[4096,8192]{1,0:T(8,128)(2,1)}) %all-gather.2.cloned.1.call-update) | async-done | bytes 67108880 | tf_op jit(solution)/shard_map/all_gather | solution.py:12
  321.4 79.6 %fusion.17 = bf16[4096,8,128]{2,0,1:T(8,128)(2,1)} fusion(bf16[8192,8,128]{2,1,0:T(8,128)(2,1)} %param.8, bf16[4096,8192]{1,0:T(8,128)(2,1)} %all-gather.2.cloned.1.call-done), kind=kOutput, calls=%fused_computation.15 | convolution fusion | flops 68723671040 | bytes 92274688 | tf_op jit(solution)/shard_map/td,dhk->thk/dot_general | solution.py:14
  401.0 10.3 %copy.12 = bf16[4096,8,128]{2,1,0:T(8,128)(2,1)} copy(bf16[4096,8,128]{2,0,1:T(8,128)(2,1)} %fusion.17) | data formatting | bytes 16777216
  411.3 79.6 %fusion.12 = bf16[4096,8,128]{2,0,1:T(8,128)(2,1)} fusion(bf16[8192,8,128]{2,1,0:T(8,128)(2,1)} %param.7, bf16[4096,8192]{1,0:T(8,128)(2,1)} %all-gather.2.cloned.1.call-done), kind=kOutput, calls=%fused_computation.14 | convolution fusion | flops 68723671040 | bytes 92274688 | tf_op jit(solution)/shard_map/td,dhk->thk/dot_general | solution.py:13
  491.0 10.3 %copy.11 = bf16[4096,8,128]{2,1,0:T(8,128)(2,1)} copy(bf16[4096,8,128]{2,0,1:T(8,128)(2,1)} %fusion.12) | data formatting | bytes 16777216
  501.3 79.6 %fusion.22 = bf16[4096,8,128]{2,0,1:T(8,128)(2,1)} fusion(bf16[8192,8,128]{2,1,0:T(8,128)(2,1)} %param.9, bf16[4096,8192]{1,0:T(8,128)(2,1)} %all-gather.2.cloned.1.call-done), kind=kOutput, calls=%fused_computation.16 | convolution fusion | flops 68723671040 | bytes 92274688 | tf_op jit(solution)/shard_map/td,dhk->thk/dot_general | solution.py:15
  580.9 10.3 %copy.13 = bf16[4096,8,128]{2,1,0:T(8,128)(2,1)} copy(bf16[4096,8,128]{2,0,1:T(8,128)(2,1)} %fusion.22) | data formatting | bytes 16777216
  (1 shorter events, 0.0 us)
Async XLA Ops:
  7.2 314.2 %all-gather.2.cloned.1.call-start = ((), (), s32[]{:S(2)}) async-start(), calls=%async_computation | async-start | bytes 75497472 | tf_op jit(solution)/shard_map/all_gather | solution.py:12
Sparse Core Ops, SparseCore 0:
  22.6 298.7 all-gather.1
where the time goes:
time: 598 us
  waiting for transfers between devices  299 us (50%)
  matrix products  239 us (40%)
  local copies, waits for them, and re-layouts  31 us (5%)
  other arithmetic  15.1 us (3%)
  between operations  14.1 us (2%)
    all_gather x1, waiting for transfers between devices, local_step(): gathered = lax.all_gather(normed, 'tp', axis=0, tiled=True)  299 us
    dot_general x1, matrix products, local_step(): jnp.einsum('td,dhk->thk', gathered, wv_local, preferred_element_type=jnp....  79.6 us
    dot_general x1, matrix products, local_step(): jnp.einsum('td,dhk->thk', gathered, wk_local, preferred_element_type=jnp....  79.6 us
    dot_general x1, matrix products, local_step(): jnp.einsum('td,dhk->thk', gathered, wq_local, preferred_element_type=jnp....  79.6 us
    unnamed x3, local copies, waits for them, and re-layouts  31 us
  transfers between devices with their start and end apart: 1, of which 1 were waited for; matrix products, arithmetic and copies ran while one was open for 0% of the time, Pallas kernels for 0%

commit v1 on v0

v1 whole, which is shorter than its diff:
```python
import functools

import jax
import jax.numpy as jnp
from jax import lax
from jax.experimental import pallas as pl
from jax.experimental.pallas import tpu as pltpu
from jax.sharding import PartitionSpec as P

F32, BF16 = jnp.float32, jnp.bfloat16
MESH_ID = pl.DeviceIdType.MESH

UNIT = 256
PIECE = 64
KC = 2048
SUB = 32
WB = 256


def fused_kernel(n, x_hbm, gain, wq, wk, wv, q_out, k_out, v_out, gathered,
                 w2, acc, xt, st, ost, wst, xin, nout,
                 in_sem, wb_sem, w_sem, load_sem, out_sem,
                 own_send, own_recv, ici_send, ici_recv, d2d_send, d2d_recv):
    rows, dim = x_hbm.shape
    half = rows // 2
    n_heads, head = wq.shape[1], wq.shape[2]
    width = n_heads * head
    chips = n // 2
    nk = dim // KC
    per_half = half // PIECE
    stage_len = per_half * nk
    n_chunks = 3 * stage_len
    own_units = rows // UNIT
    n_units = n * rows // UNIT
    local_units = 2 * own_units
    n_steps = n_units * nk
    weights, outs = (wq, wk, wv), (q_out, k_out, v_out)

    me = lax.axis_index("tp")
    chip, lane = me // 2, me % 2
    sib_lane = 1 - lane
    sibling = chip * 2 + sib_lane
    ahead = (chip + 1) % chips
    behind = (chip + chips - 1) % chips
    dest = (ahead * 2 + lane, behind * 2 + lane)

    def src_row(direction, of_lane, stage, piece):
        dist = 1 + stage // 2
        if direction == 0:
            src, part = (chip + chips - dist) % chips, stage % 2
        else:
            src, part = (chip + dist) % chips, 1 - stage % 2
        return pl.multiple_of((src * 2 + of_lane) * rows + part * half + piece * PIECE, PIECE)

    def own_row(direction, stage, piece):
        part = stage % 2 if direction == 0 else 1 - stage % 2
        return pl.multiple_of(me * rows + part * half + piece * PIECE, PIECE)

    def block(row, kc):
        return gathered.at[pl.ds(row, PIECE), pl.ds(pl.multiple_of(kc * KC, KC), KC)]

    def ici_copy(direction, row, kc, m):
        return pltpu.make_async_remote_copy(
            src_ref=block(row, kc), dst_ref=block(row, kc),
            send_sem=ici_send.at[direction, m], recv_sem=ici_recv.at[direction, m],
            device_id={"tp": dest[direction]}, device_id_type=MESH_ID)

    def d2d_copy(direction, row, kc, m):
        return pltpu.make_async_remote_copy(
            src_ref=block(row, kc), dst_ref=block(row, kc),
            send_sem=d2d_send.at[direction, m], recv_sem=d2d_recv.at[direction, m],
            device_id={"tp": sibling}, device_id_type=MESH_ID)

    def own_copy(owner, idx):
        part, piece = idx % 2, idx // 2
        ref = gathered.at[pl.ds(pl.multiple_of(owner * rows + part * half + piece * PIECE, PIECE), PIECE)]
        return pltpu.make_async_remote_copy(
            src_ref=ref, dst_ref=ref, send_sem=own_send.at[idx], recv_sem=own_recv.at[idx],
            device_id={"tp": sibling}, device_id_type=MESH_ID)

    n_wb = dim // WB

    def w_copy(p, kb, slot):
        buf = (ost, wst)[slot]
        return pltpu.make_async_copy(weights[p].at[pl.ds(pl.multiple_of(kb * WB, WB), WB)], buf.at[p], w_sem.at[slot, p])

    for slot in range(2):
        for p in range(3):
            w_copy(p, slot, slot).start()

    n_pieces = rows // PIECE

    def sub_row(idx, t):
        return pl.multiple_of((idx % 2) * half + (idx // 2) * PIECE + t * SUB, SUB)

    def x_copy(idx, t):
        return pltpu.make_async_copy(x_hbm.at[pl.ds(sub_row(idx, t), SUB)], xin.at[t], in_sem.at[t])

    def n_copy(idx, t):
        row = pl.multiple_of(me * rows + sub_row(idx, t), SUB)
        return pltpu.make_async_copy(nout.at[t], gathered.at[pl.ds(row, SUB)], wb_sem.at[t])

    for t in range(2):
        x_copy(0, t).start()

    barrier = pltpu.get_barrier_semaphore()
    for peer in (dest[0], dest[1], sibling):
        pl.semaphore_signal(barrier, inc=1, device_id={"tp": peer}, device_id_type=MESH_ID)
    pl.semaphore_wait(barrier, 3)

    cw = 1024

    def normalize(t):
        for r in range(0, SUB, 16):
            sq = jnp.zeros((16, cw), F32)
            for c in range(0, dim, cw):
                xv = xin[t, r:r + 16, c:c + cw].astype(F32)
                sq = sq + xv * xv
            scale = lax.rsqrt(jnp.sum(sq, axis=-1, keepdims=True) * (1.0 / dim) + 1e-6)
            for c in range(0, dim, cw):
                xv = xin[t, r:r + 16, c:c + cw].astype(F32)
                nout[t, r:r + 16, c:c + cw] = (xv * scale * gain[:, c:c + cw]).astype(BF16)

    def send_piece(idx):
        own_copy(me, idx).start()
        piece = idx // 2
        for direction in range(2):
            @pl.when(idx % 2 == direction)
            def _():
                for kc in range(nk):
                    ici_copy(direction, own_row(direction, 0, piece), kc, piece * nk + kc).start()

    def norm_step(idx, _):
        for t in range(2):
            @pl.when(idx > 0)
            def _():
                n_copy(idx - 1, t).wait()
                if t == 1:
                    send_piece(idx - 1)

            @pl.when(idx < n_pieces)
            def _():
                x_copy(idx, t).wait()
                normalize(t)

                @pl.when(idx + 1 < n_pieces)
                def _():
                    x_copy(idx + 1, t).start()
                n_copy(idx, t).start()
        return 0

    lax.fori_loop(0, n_pieces + 1, norm_step, 0)

    def unit_rows(t, emit):
        @pl.when(t < own_units)
        def _():
            emit([pl.multiple_of(me * rows + t * UNIT + i * PIECE, PIECE) for i in range(4)])

        @pl.when(jnp.logical_and(t >= own_units, t < local_units))
        def _():
            emit([pl.multiple_of(sibling * rows + (t - own_units) * UNIT + i * PIECE, PIECE) for i in range(4)])

        @pl.when(t >= local_units)
        def _():
            u = t - local_units
            stage, piece = u // per_half, u % per_half
            emit([src_row(d, w, stage, piece) for w in (lane, sib_lane) for d in range(2)])

    def load(s, start):
        t, kc, slot = s // nk, s % nk, s % 2
        if start:
            @pl.when(jnp.logical_and(jnp.logical_and(t >= own_units, t < local_units), kc == 0))
            def _():
                for piece in range(per_half):
                    own_copy(sibling, piece * 2 + (t - own_units)).wait_recv()

            @pl.when(t >= local_units)
            def _():
                u = t - local_units
                for d in range(2):
                    d2d_copy(d, src_row(d, sib_lane, u // per_half, u % per_half), kc, u * nk + kc).wait_recv()

            def emit(row_list):
                for i, row in enumerate(row_list):
                    pltpu.make_async_copy(block(row, kc), xt.at[slot, pl.ds(i * PIECE, PIECE)], load_sem.at[slot, i]).start()
            unit_rows(t, emit)
        else:
            for i in range(4):
                pltpu.make_async_copy(block(0, 0), xt.at[slot, pl.ds(i * PIECE, PIECE)], load_sem.at[slot, i]).wait()

    def handle(m, _):
        u, kc = m // nk, m % nk
        stage, piece = u // per_half, u % per_half
        for d in range(2):
            row = src_row(d, lane, stage, piece)
            ici_copy(d, row, kc, m).wait_recv()
            d2d_copy(d, row, kc, m).start()

            @pl.when(stage == 0)
            def _():
                ici_copy(d, own_row(d, 1, piece), kc, m + stage_len).start()

            @pl.when(stage == 1)
            def _():
                ici_copy(d, src_row(d, lane, 0, piece), kc, m + stage_len).start()
        return 0

    def handled(s):
        return jnp.minimum(n_chunks, jnp.maximum(s - (local_units * nk - 2), 4 + (2 * s) // 3))

    load(0, True)

    def relayout(i, _):
        for slot in range(2):
            kb = 2 * i + slot
            buf = (ost, wst)[slot]
            for p in range(3):
                w_copy(p, kb, slot).wait()
                tmp = st.at[p % 2]
                tmp[...] = buf[p].astype(F32).reshape(WB * n_heads, head)
                for h in range(n_heads):
                    w2[pl.ds(pl.multiple_of(kb * WB, WB), WB), p * width + h * head:p * width + (h + 1) * head] = (
                        tmp[pl.ds(h, WB, stride=n_heads), :].astype(BF16))

                @pl.when(kb + 2 < n_wb)
                def _():
                    w_copy(p, kb + 2, slot).start()
        return 0

    lax.fori_loop(0, n_wb // 2, relayout, 0)

    def before(s):
        lax.fori_loop(jnp.where(s == 0, 0, handled(s - 1)), handled(s), handle, 0)

        @pl.when(s + 1 < n_steps)
        def _():
            load(s + 1, True)
        load(s, False)

    def product(s, kc, p):
        depth = pl.ds(pl.multiple_of(kc * KC, KC), KC)
        return jnp.dot(xt[s % 2], w2[depth, p * width:(p + 1) * width], preferred_element_type=F32)

    def store(t, wait):
        if wait:
            for p in range(3):
                for i in range(4):
                    pltpu.make_async_copy(ost.at[p, pl.ds(i * PIECE, PIECE)], outs[p].at[pl.ds(0, PIECE)], out_sem.at[p, i]).wait()
        else:
            def emit(row_list):
                for p in range(3):
                    for i, row in enumerate(row_list):
                        pltpu.make_async_copy(ost.at[p, pl.ds(i * PIECE, PIECE)], outs[p].at[pl.ds(row, PIECE)], out_sem.at[p, i]).start()
            unit_rows(t, emit)

    def unit(t, _):
        def partial_step(kc, _):
            s = t * nk + kc
            before(s)
            for p in range(3):
                cols = slice(p * width, (p + 1) * width)
                acc[:, cols] = jnp.where(kc == 0, 0.0, acc[:, cols]) + product(s, kc, p)
            return 0

        lax.fori_loop(0, nk - 1, partial_step, 0)
        s = t * nk + nk - 1
        before(s)

        @pl.when(t > 0)
        def _():
            store(t - 1, True)
        for p in range(3):
            total = acc[:, p * width:(p + 1) * width] + product(s, nk - 1, p)
            tmp = st.at[p % 2]
            for h in range(n_heads):
                tmp[pl.ds(h, UNIT, stride=n_heads), :] = total[:, h * head:(h + 1) * head]
            ost[p] = tmp[...].reshape(UNIT, n_heads, head).astype(BF16)
        store(t, False)
        return 0

    lax.fori_loop(0, n_units, unit, 0)
    store(n_units - 1, True)

    def drain(m, _):
        for d in range(2):
            ici_copy(d, 0, 0, m).wait_send()
            d2d_copy(d, 0, 0, m).wait_send()
        return 0

    lax.fori_loop(0, n_chunks, drain, 0)

    def drain_own(idx, _):
        own_copy(me, idx).wait_send()
        return 0

    lax.fori_loop(0, n_pieces, drain_own, 0)


def solution(mesh):
    n = mesh.shape["tp"]

    def local_step(hidden_blk, norm_gain, wq_local, wk_local, wv_local):
        rows, dim = hidden_blk.shape
        n_heads, head = wq_local.shape[1:]
        width = n_heads * head
        chunks = 3 * (rows // 2 // PIECE) * (dim // KC)
        out = jax.ShapeDtypeStruct((n * rows, n_heads, head), BF16)
        dma = pltpu.SemaphoreType.DMA
        hbm = pl.BlockSpec(memory_space=pl.ANY)
        q, k, v, _ = pl.pallas_call(
            functools.partial(fused_kernel, n),
            out_shape=(out, out, out, jax.ShapeDtypeStruct((n * rows, dim), BF16)),
            in_specs=[hbm, pl.BlockSpec(memory_space=pltpu.VMEM), hbm, hbm, hbm],
            out_specs=(hbm, hbm, hbm, hbm),
            scratch_shapes=[
                pltpu.VMEM((dim, 3 * width), BF16),
                pltpu.VMEM((UNIT, 3 * width), F32),
                pltpu.VMEM((2, UNIT, KC), BF16),
                pltpu.VMEM((2, UNIT * n_heads, head), F32),
                pltpu.VMEM((3, UNIT, n_heads, head), BF16),
                pltpu.VMEM((3, WB, n_heads, head), BF16),
                pltpu.VMEM((2, SUB, dim), BF16),
                pltpu.VMEM((2, SUB, dim), BF16),
                dma((2,)), dma((2,)), dma((2, 3)), dma((2, 4)), dma((3, 4)),
                dma((rows // PIECE,)), dma((rows // PIECE,)),
                dma((2, chunks)), dma((2, chunks)), dma((2, chunks)), dma((2, chunks)),
            ],
            compiler_params=pltpu.CompilerParams(
                collective_id=0, has_side_effects=True, vmem_limit_bytes=67043328),
            name="norm_gather_project",
        )(hidden_blk, norm_gain.reshape(1, dim), wq_local, wk_local, wv_local)
        return q, k, v

    row_spec = P(("dp", "tp"), None)
    head_spec = P(None, "tp", None)
    out_spec = P("dp", "tp", None)
    return jax.shard_map(local_step, mesh=mesh, in_specs=(row_spec, P(None), head_spec, head_spec, head_spec), out_specs=(out_spec, out_spec, out_spec), check_vma=False)
```

time: 598 us -> 319 us (0.53)
  Pallas kernels: 0 us -> 300 us
  waiting for transfers between devices: 299 us -> 0 us
  matrix products: 239 us -> 0 us
  other arithmetic: 15.1 us -> 0.01 us
  between operations: 14.1 us -> 0.66 us
  local copies, waits for them, and re-layouts: 31 us -> 17.8 us
    pallas_call x0 -> x1, Pallas kernels: none -> 300 us  [local_step(): pl.pallas_call(functools.partial(fused_kernel, n), out_shape=(out, out, o...]
    all_gather x1 -> x0, waiting for transfers between devices: 299 us -> none  [local_step(): gathered = lax.all_gather(normed, 'tp', axis=0, tiled=True)]
    dot_general x3 -> x0, matrix products: 239 us -> none  [the longest x1 79.6 us: local_step(): jnp.einsum('td,dhk->thk', gathered, wv_local, preferred_element_type=jnp....]
    unnamed x3 -> x9, local copies, waits for them, and re-layouts: 31 us -> 17.8 us
    convert_element_type x1 -> x0, other arithmetic: 10 us -> none  [local_step(): (hidden_f32 * lax.rsqrt(mean_sq + 1e-06) * norm_gain).astype(jnp.bfloat16)]
  transfers between devices with their start and end apart: 1 -> 0, of which waited for: 1 -> 0; matrix products, arithmetic and copies ran while one was open for 0% -> 0% of each run, Pallas kernels for 0% -> 0%
where the time goes in v1:
time: 319 us; the launch traced here: 318 us
  Pallas kernels  300 us (94%)
  local copies, waits for them, and re-layouts  17.8 us (6%)
    pallas_call x1, Pallas kernels, local_step(): pl.pallas_call(functools.partial(fused_kernel, n), out_shape=(out, out, o...  300 us
    unnamed x9, local copies, waits for them, and re-layouts  17.8 us

profile of v1, /device:TPU:81, one launch (start us, length us, event | category | flops | bytes accessed | tf_op | source)
XLA Modules:
  0.0 318.3 jit_solution(14059398059255517252)
XLA Ops:
  0.6 299.8 %norm_gather_project.1 = (bf16[4096,8,128]{2,1,0:T(8,128)(2,1)}, bf16[4096,8,128]{2,1,0:T(8,128)(2,1)}, bf16[4096,8,128]{2,1,0:T(8,128)(2,1)}, bf16[4096,8192]{1,0:T(8,128)(2,1)}) custom-call(bf16[512,8192]{1,0:T(8,128)(2,1)} %x_hbm.1, f32[1,8192]{1,0:T(1,128)} %bitcast.3, bf16[8192,8,128]{2,1,0:T(8,128)(2,1)} %wq.1, bf16[8192,8,128]{2,1,0:T(8,128)(2,1)} %wk.1, ...), custom_call_target="tpu_custom_call" | custom-call | tf_op jit(solution)/shard_map/norm_gather_project/pallas_call | solution.py:310
  300.4 0.0 copy-start
  300.4 0.0 slice-start
  300.4 8.2 %copy.11 = bf16[4096,8,128]{2,1,0:T(8,128)(2,1)} copy(bf16[4096,8,128]{2,1,0:T(8,128)(2,1)} %get-tuple-element.12) | data formatting | bytes 16777216
  308.6 0.2 copy-done
  308.8 0.0 slice-start.1
  308.8 4.3 %copy.12 = bf16[4096,8,128]{2,1,0:T(8,128)(2,1)} copy(bf16[4096,8,128]{2,1,0:T(8,128)(2,1)S(1)} %copy-done) | data formatting | bytes 16777216
  313.0 0.0 slice-done
  313.0 1.8 slice-done.1
  314.9 3.4 %copy.13 = bf16[4096,8,128]{2,1,0:T(8,128)(2,1)} copy(bf16[4096,8,128]{2,1,0:T(8,128)(2,1)S(1)} %bitcast.2) | data formatting | bytes 16777216
  (1 shorter events, 0.0 us)
Async XLA Ops:
  300.4 8.3 %copy-start = (bf16[4096,8,128]{2,1,0:T(8,128)(2,1)S(1)}, bf16[4096,8,128]{2,1,0:T(8,128)(2,1)}, u32[]{:S(2)}) copy-start(bf16[4096,8,128]{2,1,0:T(8,128)(2,1)} %get-tuple-element.13) | copy-start | bytes 25165828
  300.4 12.6 %slice-start = ((s8[8388608]{0:T(1024)(128)(4,1)}), s8[4194304]{0:T(1024)(128)(4,1)S(1)}, s32[]{:S(2)}) async-start(s8[8388608]{0:T(1024)(128)(4,1)} %bitcast.1), calls=%async_computation | async-start | bytes 8388608
  308.8 6.1 %slice-start.1 = ((s8[8388608]{0:T(1024)(128)(4,1)}), s8[4194304]{0:T(1024)(128)(4,1)S(1)}, s32[]{:S(2)}) async-start(s8[8388608]{0:T(1024)(128)(4,1)} %bitcast.1), calls=%async_computation.1 | async-start | bytes 8388608

commit v2 on v1

--- a/solution.py
+++ b/solution.py
@@ -17,8 +17,8 @@
 WB = 256
 
 
-def fused_kernel(n, x_hbm, gain, wq, wk, wv, q_out, k_out, v_out, gathered,
-                 w2, acc, xt, st, ost, wst, xin, nout,
+def fused_kernel(n, x_hbm, gain, wq, wk, wv, q_out, k_out, v_out, gathered, w2,
+                 acc, xt, st, ost, wst, xin, nout,
                  in_sem, wb_sem, w_sem, load_sem, out_sem,
                  own_send, own_recv, ici_send, ici_recv, d2d_send, d2d_recv):
     rows, dim = x_hbm.shape
@@ -31,7 +31,7 @@
     stage_len = per_half * nk
     n_chunks = 3 * stage_len
     own_units = rows // UNIT
-    n_units = n * rows // UNIT
+    n_units = n * rows // UNIT - 1
     local_units = 2 * own_units
     n_steps = n_units * nk
     weights, outs = (wq, wk, wv), (q_out, k_out, v_out)
@@ -84,24 +84,23 @@
         buf = (ost, wst)[slot]
         return pltpu.make_async_copy(weights[p].at[pl.ds(pl.multiple_of(kb * WB, WB), WB)], buf.at[p], w_sem.at[slot, p])
 
+    n_pieces = rows // PIECE
+
+    def sub_row(idx, t):
+        return pl.multiple_of((idx % 2) * half + (idx // 2) * PIECE + t * SUB, SUB)
+
+    def x_copy(idx, t):
+        return pltpu.make_async_copy(x_hbm.at[pl.ds(sub_row(idx, t), SUB)], xin.at[t], in_sem.at[t])
+
+    def n_copy(idx, t):
+        row = pl.multiple_of(me * rows + sub_row(idx, t), SUB)
+        return pltpu.make_async_copy(nout.at[t], gathered.at[pl.ds(row, SUB)], wb_sem.at[t])
+
+    for t in range(2):
+        x_copy(0, t).start()
     for slot in range(2):
         for p in range(3):
             w_copy(p, slot, slot).start()
-
-    n_pieces = rows // PIECE
-
-    def sub_row(idx, t):
-        return pl.multiple_of((idx % 2) * half + (idx // 2) * PIECE + t * SUB, SUB)
-
-    def x_copy(idx, t):
-        return pltpu.make_async_copy(x_hbm.at[pl.ds(sub_row(idx, t), SUB)], xin.at[t], in_sem.at[t])
-
-    def n_copy(idx, t):
-        row = pl.multiple_of(me * rows + sub_row(idx, t), SUB)
-        return pltpu.make_async_copy(nout.at[t], gathered.at[pl.ds(row, SUB)], wb_sem.at[t])
-
-    for t in range(2):
-        x_copy(0, t).start()
 
     barrier = pltpu.get_barrier_semaphore()
     for peer in (dest[0], dest[1], sibling):
@@ -206,7 +205,7 @@
         return 0
 
     def handled(s):
-        return jnp.minimum(n_chunks, jnp.maximum(s - (local_units * nk - 2), 4 + (2 * s) // 3))
+        return jnp.minimum(n_chunks - nk, jnp.maximum(s - (local_units * nk - 2), 4 + (2 * s) // 3))
 
     load(0, True)
 
@@ -281,6 +280,11 @@
     lax.fori_loop(0, n_units, unit, 0)
     store(n_units - 1, True)
 
+    lax.fori_loop(n_chunks - nk, n_chunks, handle, 0)
+    for kc in range(nk):
+        for d in range(2):
+            d2d_copy(d, src_row(d, sib_lane, 2, per_half - 1), kc, n_chunks - nk + kc).wait_recv()
+
     def drain(m, _):
         for d in range(2):
             ici_copy(d, 0, 0, m).wait_send()
@@ -294,6 +298,95 @@
         return 0
 
     lax.fori_loop(0, n_pieces, drain_own, 0)
+
+
+def finish_kernel(n, w2, gathered, q_in, k_in, v_in, q_out, k_out, v_out,
+                  acc, xt, st, ost, buf, load_sem, read_sem, write_sem, out_sem):
+    ins, outs = (q_in, k_in, v_in), (q_out, k_out, v_out)
+    total_rows, dim = gathered.shape
+    rows = total_rows // n
+    half = rows // 2
+    n_heads, head = q_in.shape[1], q_in.shape[2]
+    width = n_heads * head
+    chips = n // 2
+    nk = dim // KC
+    chip_rows = 2 * rows
+
+    far = (lax.axis_index("tp") // 2 + chips // 2) % chips
+    unit_rows = [pl.multiple_of(far * chip_rows + end - PIECE, PIECE) for end in range(half, chip_rows + 1, half)]
+    moves = []
+    for other in range(1, chips):
+        base = ((far + other) % chips) * chip_rows
+        moves += [(pl.multiple_of(base + r, UNIT), UNIT) for r in range(0, chip_rows, UNIT)]
+    moves += [(pl.multiple_of(far * chip_rows + r, UNIT), half - PIECE) for r in range(0, chip_rows, half)]
+
+    def read(j):
+        row, size = moves[j]
+        return [pltpu.make_async_copy(ins[p].at[pl.ds(row, size)], buf.at[j % 3, p, pl.ds(0, size)], read_sem.at[j % 3, p]) for p in range(3)]
+
+    def write(j):
+        row, size = moves[j]
+        return [pltpu.make_async_copy(buf.at[j % 3, p, pl.ds(0, size)], outs[p].at[pl.ds(row, size)], write_sem.at[j % 3, p]) for p in range(3)]
+
+    def tick(j):
+        if 0 <= j - 3 < len(moves):
+            for c in write(j - 3):
+                c.wait()
+        if 0 <= j < len(moves):
+            for c in read(j):
+                c.start()
+        if 0 <= j - 1 < len(moves):
+            for c in read(j - 1):
+                c.wait()
+            for c in write(j - 1):
+                c.start()
+
+    def load(kc):
+        return [pltpu.make_async_copy(
+            gathered.at[pl.ds(row, PIECE), pl.ds(kc * KC, KC)], xt.at[kc % 2, pl.ds(i * PIECE, PIECE)], load_sem.at[kc % 2, i])
+            for i, row in enumerate(unit_rows)]
+
+    def result(p):
+        return [pltpu.make_async_copy(ost.at[p, pl.ds(i * PIECE, PIECE)], outs[p].at[pl.ds(row, PIECE)], out_sem.at[p, i])
+                for i, row in enumerate(unit_rows)]
+
+    for kc in range(min(2, nk)):
+        for c in load(kc):
+            c.start()
+    ticks = len(moves) + 3
+    done = 2
+    for j in range(done):
+        tick(j)
+    n_dots = 3 * nk
+    for kc in range(nk):
+        for c in load(kc):
+            c.wait()
+        for p in range(3):
+            cols = slice(p * width, (p + 1) * width)
+            part = jnp.dot(xt[kc % 2], w2[kc * KC:(kc + 1) * KC, cols], preferred_element_type=F32)
+            if kc > 0:
+                part = acc[:, cols] + part
+            if kc < nk - 1:
+                acc[:, cols] = part
+            else:
+                tmp = st.at[p % 2]
+                for h in range(n_heads):
+                    tmp[pl.ds(h, UNIT, stride=n_heads), :] = part[:, h * head:(h + 1) * head]
+                ost[p] = tmp[...].reshape(UNIT, n_heads, head).astype(BF16)
+                for c in result(p):
+                    c.start()
+            upto = 2 + (kc * 3 + p + 1) * (ticks - 3) // n_dots
+            for j in range(done, upto):
+                tick(j)
+            done = upto
+        if kc + 2 < nk:
+            for c in load(kc + 2):
+                c.start()
+    for j in range(done, ticks):
+        tick(j)
+    for p in range(3):
+        for c in result(p):
+            c.wait()
 
 
 def solution(mesh):
@@ -307,13 +400,14 @@
         out = jax.ShapeDtypeStruct((n * rows, n_heads, head), BF16)
         dma = pltpu.SemaphoreType.DMA
         hbm = pl.BlockSpec(memory_space=pl.ANY)
-        q, k, v, _ = pl.pallas_call(
+        vmem = pl.BlockSpec(memory_space=pltpu.VMEM)
+        room = 67043328 - 2 * dim * 3 * width
+        q, k, v, gathered, w2 = pl.pallas_call(
             functools.partial(fused_kernel, n),
-            out_shape=(out, out, out, jax.ShapeDtypeStruct((n * rows, dim), BF16)),
-            in_specs=[hbm, pl.BlockSpec(memory_space=pltpu.VMEM), hbm, hbm, hbm],
-            out_specs=(hbm, hbm, hbm, hbm),
+            out_shape=(out, out, out, jax.ShapeDtypeStruct((n * rows, dim), BF16), pltpu.VMEM((dim, 3 * width), BF16)),
+            in_specs=[hbm, vmem, hbm, hbm, hbm],
+            out_specs=(hbm, hbm, hbm, hbm, vmem),
             scratch_shapes=[
-                pltpu.VMEM((dim, 3 * width), BF16),
                 pltpu.VMEM((UNIT, 3 * width), F32),
                 pltpu.VMEM((2, UNIT, KC), BF16),
                 pltpu.VMEM((2, UNIT * n_heads, head), F32),
@@ -326,10 +420,25 @@
                 dma((2, chunks)), dma((2, chunks)), dma((2, chunks)), dma((2, chunks)),
             ],
             compiler_params=pltpu.CompilerParams(
-                collective_id=0, has_side_effects=True, vmem_limit_bytes=67043328),
+                collective_id=0, has_side_effects=True, vmem_limit_bytes=room),
             name="norm_gather_project",
         )(hidden_blk, norm_gain.reshape(1, dim), wq_local, wk_local, wv_local)
-        return q, k, v
+        return pl.pallas_call(
+            functools.partial(finish_kernel, n),
+            out_shape=(out, out, out),
+            in_specs=[vmem, hbm, hbm, hbm, hbm],
+            out_specs=(hbm, hbm, hbm),
+            scratch_shapes=[
+                pltpu.VMEM((UNIT, 3 * width), F32),
+                pltpu.VMEM((2, UNIT, KC), BF16),
+                pltpu.VMEM((2, UNIT * n_heads, head), F32),
+                pltpu.VMEM((3, UNIT, n_heads, head), BF16),
+                pltpu.VMEM((3, 3, UNIT, n_heads, head), BF16),
+                dma((2, 4)), dma((3, 3)), dma((3, 3)), dma((3, 4)),
+            ],
+            compiler_params=pltpu.CompilerParams(vmem_limit_bytes=room),
+            name="finish",
+        )(pltpu.with_memory_space_constraint(w2, pltpu.VMEM), gathered, q, k, v)
 
     row_spec = P(("dp", "tp"), None)
     head_spec = P(None, "tp", None)

time: 319 us -> 311 us (0.975)
  local copies, waits for them, and re-layouts: 17.8 us -> 0 us
  Pallas kernels: 300 us -> 309 us
    pallas_call x0 -> x1, Pallas kernels: none -> 24.4 us  [local_step(): pl.pallas_call(functools.partial(finish_kernel, n), out_shape=(out, out,...]
    unnamed x9 -> x0, local copies, waits for them, and re-layouts: 17.8 us -> none
    pallas_call x1, Pallas kernels: 300 us -> 285 us  [local_step(): pl.pallas_call(functools.partial(fused_kernel, n), out_shape=(out, out, o...]
where the time goes in v2:
time: 311 us; the launch traced here: 310 us
  Pallas kernels  309 us (99%)
    pallas_call x1, Pallas kernels, local_step(): pl.pallas_call(functools.partial(fused_kernel, n), out_shape=(out, out, o...  285 us
    pallas_call x1, Pallas kernels, local_step(): pl.pallas_call(functools.partial(finish_kernel, n), out_shape=(out, out,...  24.4 us

profile of v2, /device:TPU:81, one launch (start us, length us, event | category | flops | bytes accessed | tf_op | source)
XLA Modules:
  0.0 310.1 jit_solution(13467447931227779108)
XLA Ops:
  0.6 284.9 %norm_gather_project.1 = (bf16[4096,8,128]{2,1,0:T(8,128)(2,1)}, bf16[4096,8,128]{2,1,0:T(8,128)(2,1)}, bf16[4096,8,128]{2,1,0:T(8,128)(2,1)}, bf16[4096,8192]{1,0:T(8,128)(2,1)}, bf16[8192,3072]{1,0:T(8,128)(2,1)S(1)}) custom-call(bf16[512,8192]{1,0:T(8,128)(2,1)} %x_hbm.1, f32[1,8192]{1,0:T(1,128)} %bitcast.1, bf16[8192,8,128]{2,1,0:T(8,128)(2,1)} %wq.1, ...), custom_call_target="tpu_custom_call" | custom-call | tf_op jit(solution)/shard_map/norm_gather_project/pallas_call | solution.py:405
  285.5 24.4 %finish.1 = (bf16[4096,8,128]{2,1,0:T(8,128)(2,1)}, bf16[4096,8,128]{2,1,0:T(8,128)(2,1)}, bf16[4096,8,128]{2,1,0:T(8,128)(2,1)}) custom-call(bf16[8192,3072]{1,0:T(8,128)(2,1)S(1)} %get-tuple-element.8.w2, bf16[4096,8192]{1,0:T(8,128)(2,1)} %get-tuple-element.9.gathered, bf16[4096,8,128]{2,1,0:T(8,128)(2,1)} %get-tuple-element.10.q_in, ...), custom_call_target="tpu_custom_call" | custom-call | tf_op jit(solution)/shard_map/finish/pallas_call | solution.py:426

commit v3 on v1

--- a/solution.py
+++ b/solution.py
@@ -13,12 +13,15 @@
 UNIT = 256
 PIECE = 64
 KC = 2048
+SLOTS = 10
+SPAN = 128
+FIRST_READS = 3
 SUB = 32
 WB = 256
 
 
-def fused_kernel(n, x_hbm, gain, wq, wk, wv, q_out, k_out, v_out, gathered,
-                 w2, acc, xt, st, ost, wst, xin, nout,
+def fused_kernel(n, x_hbm, gain, wq, wk, wv, q_out, k_out, v_out, gathered, w2,
+                 acc, xt, st, ost, wst, xin,
                  in_sem, wb_sem, w_sem, load_sem, out_sem,
                  own_send, own_recv, ici_send, ici_recv, d2d_send, d2d_recv):
     rows, dim = x_hbm.shape
@@ -31,7 +34,7 @@
     stage_len = per_half * nk
     n_chunks = 3 * stage_len
     own_units = rows // UNIT
-    n_units = n * rows // UNIT
+    n_units = n * rows // UNIT - 1
     local_units = 2 * own_units
     n_steps = n_units * nk
     weights, outs = (wq, wk, wv), (q_out, k_out, v_out)
@@ -84,69 +87,77 @@
         buf = (ost, wst)[slot]
         return pltpu.make_async_copy(weights[p].at[pl.ds(pl.multiple_of(kb * WB, WB), WB)], buf.at[p], w_sem.at[slot, p])
 
+    n_pieces = rows // PIECE
+
+    def sub_row(idx, t):
+        return pl.multiple_of((idx % 2) * half + (idx // 2) * PIECE + t * SUB, SUB)
+
+    def x_copy(idx, t):
+        slot = (idx % 2) * 2 + t
+        return pltpu.make_async_copy(x_hbm.at[pl.ds(sub_row(idx, t), SUB)], xin.at[slot], in_sem.at[slot])
+
+    def n_copies(idx, t):
+        row = pl.multiple_of(me * rows + sub_row(idx, t), SUB)
+        return [pltpu.make_async_copy(
+            xt.at[idx % 2, pl.ds((t * nk + kc) * SUB, SUB)],
+            gathered.at[pl.ds(row, SUB), pl.ds(kc * KC, KC)], wb_sem.at[(idx % 2) * 2 + t, kc]) for kc in range(nk)]
+
+    for idx in range(2):
+        for t in range(2):
+            x_copy(idx, t).start()
     for slot in range(2):
         for p in range(3):
             w_copy(p, slot, slot).start()
-
-    n_pieces = rows // PIECE
-
-    def sub_row(idx, t):
-        return pl.multiple_of((idx % 2) * half + (idx // 2) * PIECE + t * SUB, SUB)
-
-    def x_copy(idx, t):
-        return pltpu.make_async_copy(x_hbm.at[pl.ds(sub_row(idx, t), SUB)], xin.at[t], in_sem.at[t])
-
-    def n_copy(idx, t):
-        row = pl.multiple_of(me * rows + sub_row(idx, t), SUB)
-        return pltpu.make_async_copy(nout.at[t], gathered.at[pl.ds(row, SUB)], wb_sem.at[t])
-
-    for t in range(2):
-        x_copy(0, t).start()
 
     barrier = pltpu.get_barrier_semaphore()
     for peer in (dest[0], dest[1], sibling):
         pl.semaphore_signal(barrier, inc=1, device_id={"tp": peer}, device_id_type=MESH_ID)
     pl.semaphore_wait(barrier, 3)
 
-    cw = 1024
-
-    def normalize(t):
+    cw = min(1024, KC)
+
+    def normalize(idx, t):
+        slot = (idx % 2) * 2 + t
         for r in range(0, SUB, 16):
             sq = jnp.zeros((16, cw), F32)
             for c in range(0, dim, cw):
-                xv = xin[t, r:r + 16, c:c + cw].astype(F32)
+                xv = xin[slot, r:r + 16, c:c + cw].astype(F32)
                 sq = sq + xv * xv
             scale = lax.rsqrt(jnp.sum(sq, axis=-1, keepdims=True) * (1.0 / dim) + 1e-6)
             for c in range(0, dim, cw):
-                xv = xin[t, r:r + 16, c:c + cw].astype(F32)
-                nout[t, r:r + 16, c:c + cw] = (xv * scale * gain[:, c:c + cw]).astype(BF16)
+                xv = xin[slot, r:r + 16, c:c + cw].astype(F32)
+                first = (t * nk + c // KC) * SUB + r
+                xt[idx % 2, first:first + 16, c % KC:c % KC + cw] = (xv * scale * gain[:, c:c + cw]).astype(BF16)
 
     def send_piece(idx):
-        own_copy(me, idx).start()
         piece = idx // 2
         for direction in range(2):
             @pl.when(idx % 2 == direction)
             def _():
                 for kc in range(nk):
                     ici_copy(direction, own_row(direction, 0, piece), kc, piece * nk + kc).start()
+        own_copy(me, idx).start()
 
     def norm_step(idx, _):
         for t in range(2):
-            @pl.when(idx > 0)
-            def _():
-                n_copy(idx - 1, t).wait()
-                if t == 1:
+            @pl.when(idx < n_pieces)
+            def _():
+                x_copy(idx, t).wait()
+                normalize(idx, t)
+
+                @pl.when(idx + 2 < n_pieces)
+                def _():
+                    x_copy(idx + 2, t).start()
+                for c in n_copies(idx, t):
+                    c.start()
+
+            if t == 0:
+                @pl.when(idx > 0)
+                def _():
+                    for u in range(2):
+                        for c in n_copies(idx - 1, u):
+                            c.wait()
                     send_piece(idx - 1)
-
-            @pl.when(idx < n_pieces)
-            def _():
-                x_copy(idx, t).wait()
-                normalize(t)
-
-                @pl.when(idx + 1 < n_pieces)
-                def _():
-                    x_copy(idx + 1, t).start()
-                n_copy(idx, t).start()
         return 0
 
     lax.fori_loop(0, n_pieces + 1, norm_step, 0)
@@ -206,7 +217,7 @@
         return 0
 
     def handled(s):
-        return jnp.minimum(n_chunks, jnp.maximum(s - (local_units * nk - 2), 4 + (2 * s) // 3))
+        return jnp.minimum(n_chunks - nk, jnp.maximum(s - (local_units * nk - 2), 4 + (2 * s) // 3))
 
     load(0, True)
 
@@ -287,13 +298,126 @@
             d2d_copy(d, 0, 0, m).wait_send()
         return 0
 
-    lax.fori_loop(0, n_chunks, drain, 0)
-
     def drain_own(idx, _):
         own_copy(me, idx).wait_send()
         return 0
 
     lax.fori_loop(0, n_pieces, drain_own, 0)
+    lax.fori_loop(0, n_chunks - nk, drain, 0)
+
+    lax.fori_loop(n_chunks - nk, n_chunks, handle, 0)
+    lax.fori_loop(n_chunks - nk, n_chunks, drain, 0)
+    for kc in range(nk):
+        for d in range(2):
+            d2d_copy(d, src_row(d, sib_lane, 2, per_half - 1), kc, n_chunks - nk + kc).wait_recv()
+
+
+def finish_kernel(n, w2, gathered, q_in, k_in, v_in, q_out, k_out, v_out,
+                  xt, acc, st, ost, buf, load_sem, read_sem, write_sem, out_sem):
+    ins, outs = (q_in, k_in, v_in), (q_out, k_out, v_out)
+    total_rows, dim = gathered.shape
+    rows = total_rows // n
+    half = rows // 2
+    n_heads, head = q_in.shape[1], q_in.shape[2]
+    width = n_heads * head
+    chips = n // 2
+    chip_rows = 2 * rows
+    slots, span = buf.shape[0], buf.shape[2]
+
+    far = (lax.axis_index("tp") // 2 + chips // 2) % chips
+    unit_rows = [pl.multiple_of(far * chip_rows + end - PIECE, PIECE) for end in range(half, chip_rows + 1, half)]
+    moves = []
+    for other in range(1, chips):
+        base = ((far + other) % chips) * chip_rows
+        moves += [(pl.multiple_of(base + r, PIECE), span) for r in range(0, chip_rows, span)]
+    for part in range(0, chip_rows, half):
+        for r in range(0, half - PIECE, span):
+            moves.append((pl.multiple_of(far * chip_rows + part + r, PIECE), min(span, half - PIECE - r)))
+
+    def read(j):
+        row, size = moves[j]
+        return [pltpu.make_async_copy(ins[p].at[pl.ds(row, size)], buf.at[j % slots, p, pl.ds(0, size)], read_sem.at[j % slots, p]) for p in range(3)]
+
+    def write(j):
+        row, size = moves[j]
+        return [pltpu.make_async_copy(buf.at[j % slots, p, pl.ds(0, size)], outs[p].at[pl.ds(row, size)], write_sem.at[j % slots, p]) for p in range(3)]
+
+    def start(copies):
+        for c in copies:
+            c.start()
+
+    def wait(copies):
+        for c in copies:
+            c.wait()
+
+    deep = dim // 2
+
+    def loads(k):
+        return [pltpu.make_async_copy(
+            gathered.at[pl.ds(row, PIECE), pl.ds(k * deep, deep)],
+            xt.at[pl.ds(i * PIECE, PIECE), pl.ds(k * deep, deep)], load_sem.at[k, i]) for i, row in enumerate(unit_rows)]
+
+    def result(p):
+        return [pltpu.make_async_copy(ost.at[p, pl.ds(i * PIECE, PIECE)], outs[p].at[pl.ds(row, PIECE)], out_sem.at[p, i])
+                for i, row in enumerate(unit_rows)]
+
+    n_read, n_written, n_freed = 0, 0, 0
+    for k in range(2):
+        start(loads(k))
+    for _ in range(FIRST_READS):
+        start(read(n_read))
+        n_read += 1
+    wait(loads(0))
+    while n_read < slots:
+        start(read(n_read))
+        n_read += 1
+
+    n_cols = acc.shape[1]
+    n_dots = 2 * (3 * width // n_cols)
+    per_p = width // n_cols
+    heads = n_cols // head
+    for i_dot in range(n_dots):
+        nb, k = i_dot // 2, i_dot % 2
+        if i_dot == 1:
+            wait(loads(1))
+        part = jnp.dot(xt[:, k * deep:(k + 1) * deep], w2[k * deep:(k + 1) * deep, nb * n_cols:(nb + 1) * n_cols],
+                       preferred_element_type=F32)
+        if k == 0:
+            acc[...] = part
+        else:
+            part = acc[...] + part
+            p = nb // per_p
+            for i in range(heads):
+                st[pl.ds((nb % per_p) * heads + i, UNIT, stride=n_heads), :] = part[:, i * head:(i + 1) * head]
+            if nb % per_p == per_p - 1:
+                ost[p] = st[...].reshape(UNIT, n_heads, head).astype(BF16)
+                start(result(p))
+        free = n_written
+        target = min(len(moves), -(-len(moves) * (i_dot + 1) // (n_dots - 1)))
+        while n_written < min(target, n_read):
+            wait(read(n_written))
+            start(write(n_written))
+            n_written += 1
+        while n_freed < free:
+            wait(write(n_freed))
+            n_freed += 1
+            if n_read < len(moves):
+                start(read(n_read))
+                n_read += 1
+    while n_written < len(moves):
+        while n_freed < n_written and n_read < len(moves):
+            wait(write(n_freed))
+            n_freed += 1
+            start(read(n_read))
+            n_read += 1
+        wait(read(n_written))
+        start(write(n_written))
+        n_written += 1
+    while n_freed < len(moves):
+        wait(write(n_freed))
+        n_freed += 1
+    for p in range(3):
+        wait(result(p))
 
 
 def solution(mesh):
@@ -307,29 +431,44 @@
         out = jax.ShapeDtypeStruct((n * rows, n_heads, head), BF16)
         dma = pltpu.SemaphoreType.DMA
         hbm = pl.BlockSpec(memory_space=pl.ANY)
-        q, k, v, _ = pl.pallas_call(
+        vmem = pl.BlockSpec(memory_space=pltpu.VMEM)
+        room = 67043328 - 2 * dim * 3 * width
+        q, k, v, gathered, w2 = pl.pallas_call(
             functools.partial(fused_kernel, n),
-            out_shape=(out, out, out, jax.ShapeDtypeStruct((n * rows, dim), BF16)),
-            in_specs=[hbm, pl.BlockSpec(memory_space=pltpu.VMEM), hbm, hbm, hbm],
-            out_specs=(hbm, hbm, hbm, hbm),
+            out_shape=(out, out, out, jax.ShapeDtypeStruct((n * rows, dim), BF16), pltpu.VMEM((dim, 3 * width), BF16)),
+            in_specs=[hbm, vmem, hbm, hbm, hbm],
+            out_specs=(hbm, hbm, hbm, hbm, vmem),
             scratch_shapes=[
-                pltpu.VMEM((dim, 3 * width), BF16),
                 pltpu.VMEM((UNIT, 3 * width), F32),
                 pltpu.VMEM((2, UNIT, KC), BF16),
                 pltpu.VMEM((2, UNIT * n_heads, head), F32),
                 pltpu.VMEM((3, UNIT, n_heads, head), BF16),
                 pltpu.VMEM((3, WB, n_heads, head), BF16),
-                pltpu.VMEM((2, SUB, dim), BF16),
-                pltpu.VMEM((2, SUB, dim), BF16),
-                dma((2,)), dma((2,)), dma((2, 3)), dma((2, 4)), dma((3, 4)),
+                pltpu.VMEM((4, SUB, dim), BF16),
+                dma((4,)), dma((4, dim // KC)), dma((2, 3)), dma((2, 4)), dma((3, 4)),
                 dma((rows // PIECE,)), dma((rows // PIECE,)),
                 dma((2, chunks)), dma((2, chunks)), dma((2, chunks)), dma((2, chunks)),
             ],
             compiler_params=pltpu.CompilerParams(
-                collective_id=0, has_side_effects=True, vmem_limit_bytes=67043328),
+                collective_id=0, has_side_effects=True, vmem_limit_bytes=room),
             name="norm_gather_project",
         )(hidden_blk, norm_gain.reshape(1, dim), wq_local, wk_local, wv_local)
-        return q, k, v
+        return pl.pallas_call(
+            functools.partial(finish_kernel, n),
+            out_shape=(out, out, out),
+            in_specs=[vmem, hbm, hbm, hbm, hbm],
+            out_specs=(hbm, hbm, hbm),
+            scratch_shapes=[
+                pltpu.VMEM((UNIT, dim), BF16),
+                pltpu.VMEM((UNIT, width // 2), F32),
+                pltpu.VMEM((UNIT * n_heads, head), F32),
+                pltpu.VMEM((3, UNIT, n_heads, head), BF16),
+                pltpu.VMEM((SLOTS, 3, SPAN, n_heads, head), BF16),
+                dma((2, 4)), dma((SLOTS, 3)), dma((SLOTS, 3)), dma((3, 4)),
+            ],
+            compiler_params=pltpu.CompilerParams(vmem_limit_bytes=room),
+            name="finish",
+        )(pltpu.with_memory_space_constraint(w2, pltpu.VMEM), gathered, q, k, v)
 
     row_spec = P(("dp", "tp"), None)
     head_spec = P(None, "tp", None)

time: 319 us -> 305 us (0.956)
  local copies, waits for them, and re-layouts: 17.8 us -> 0 us
  Pallas kernels: 300 us -> 304 us
    pallas_call x0 -> x1, Pallas kernels: none -> 20.4 us  [local_step(): pl.pallas_call(functools.partial(finish_kernel, n), out_shape=(out, out,...]
    unnamed x9 -> x0, local copies, waits for them, and re-layouts: 17.8 us -> none
    pallas_call x1, Pallas kernels: 300 us -> 284 us  [local_step(): pl.pallas_call(functools.partial(fused_kernel, n), out_shape=(out, out, o...]
where the time goes in v3:
time: 305 us
  Pallas kernels  304 us (100%)
    pallas_call x1, Pallas kernels, local_step(): pl.pallas_call(functools.partial(fused_kernel, n), out_shape=(out, out, o...  284 us
    pallas_call x1, Pallas kernels, local_step(): pl.pallas_call(functools.partial(finish_kernel, n), out_shape=(out, out,...  20.4 us

profile of v3, /device:TPU:81, one launch (start us, length us, event | category | flops | bytes accessed | tf_op | source)
XLA Modules:
  0.0 305.0 jit_solution(96483919727898042)
XLA Ops:
  0.6 283.8 %norm_gather_project.1 = (bf16[4096,8,128]{2,1,0:T(8,128)(2,1)}, bf16[4096,8,128]{2,1,0:T(8,128)(2,1)}, bf16[4096,8,128]{2,1,0:T(8,128)(2,1)}, bf16[4096,8192]{1,0:T(8,128)(2,1)}, bf16[8192,3072]{1,0:T(8,128)(2,1)S(1)}) custom-call(bf16[512,8192]{1,0:T(8,128)(2,1)} %x_hbm.1, f32[1,8192]{1,0:T(1,128)} %bitcast.1, bf16[8192,8,128]{2,1,0:T(8,128)(2,1)} %wq.1, ...), custom_call_target="tpu_custom_call" | custom-call | tf_op jit(solution)/shard_map/norm_gather_project/pallas_call | solution.py:436
  284.4 20.4 %finish.1 = (bf16[4096,8,128]{2,1,0:T(8,128)(2,1)}, bf16[4096,8,128]{2,1,0:T(8,128)(2,1)}, bf16[4096,8,128]{2,1,0:T(8,128)(2,1)}) custom-call(bf16[8192,3072]{1,0:T(8,128)(2,1)S(1)} %get-tuple-element.8.w2, bf16[4096,8192]{1,0:T(8,128)(2,1)} %get-tuple-element.9.gathered, bf16[4096,8,128]{2,1,0:T(8,128)(2,1)} %get-tuple-element.10.q_in, ...), custom_call_target="tpu_custom_call" | custom-call | tf_op jit(solution)/shard_map/finish/pallas_call | solution.py:456

commit v4 on v3

--- a/solution.py
+++ b/solution.py
@@ -13,16 +13,18 @@
 UNIT = 256
 PIECE = 64
 KC = 2048
+EARLY = 2
 SLOTS = 10
+LAG = 4
 SPAN = 128
 FIRST_READS = 3
 SUB = 32
 WB = 256
 
 
-def fused_kernel(n, x_hbm, gain, wq, wk, wv, q_out, k_out, v_out, gathered, w2,
+def fused_kernel(n, x_hbm, gain, wq, wk, wv, q_out, k_out, v_out, gathered, w2, partial,
                  acc, xt, st, ost, wst, xin,
-                 in_sem, wb_sem, w_sem, load_sem, out_sem,
+                 in_sem, wb_sem, w_sem, load_sem, out_sem, partial_sem,
                  own_send, own_recv, ici_send, ici_recv, d2d_send, d2d_recv):
     rows, dim = x_hbm.shape
     half = rows // 2
@@ -36,7 +38,7 @@
     own_units = rows // UNIT
     n_units = n * rows // UNIT - 1
     local_units = 2 * own_units
-    n_steps = n_units * nk
+    n_steps = n_units * nk + EARLY
     weights, outs = (wq, wk, wv), (q_out, k_out, v_out)
 
     me = lax.axis_index("tp")
@@ -47,6 +49,10 @@
     behind = (chip + chips - 1) % chips
     dest = (ahead * 2 + lane, behind * 2 + lane)
 
+    barrier = pltpu.get_barrier_semaphore()
+    for peer in (dest[0], dest[1], sibling):
+        pl.semaphore_signal(barrier, inc=1, device_id={"tp": peer}, device_id_type=MESH_ID)
+
     def src_row(direction, of_lane, stage, piece):
         dist = 1 + stage // 2
         if direction == 0:
@@ -108,11 +114,6 @@
     for slot in range(2):
         for p in range(3):
             w_copy(p, slot, slot).start()
-
-    barrier = pltpu.get_barrier_semaphore()
-    for peer in (dest[0], dest[1], sibling):
-        pl.semaphore_signal(barrier, inc=1, device_id={"tp": peer}, device_id_type=MESH_ID)
-    pl.semaphore_wait(barrier, 3)
 
     cw = min(1024, KC)
 
@@ -138,29 +139,33 @@
                     ici_copy(direction, own_row(direction, 0, piece), kc, piece * nk + kc).start()
         own_copy(me, idx).start()
 
+    def norm_half(idx, t):
+        x_copy(idx, t).wait()
+        normalize(idx, t)
+
+        @pl.when(idx + 2 < n_pieces)
+        def _():
+            x_copy(idx + 2, t).start()
+        for c in n_copies(idx, t):
+            c.start()
+
     def norm_step(idx, _):
         for t in range(2):
             @pl.when(idx < n_pieces)
             def _():
-                x_copy(idx, t).wait()
-                normalize(idx, t)
-
-                @pl.when(idx + 2 < n_pieces)
-                def _():
-                    x_copy(idx + 2, t).start()
-                for c in n_copies(idx, t):
-                    c.start()
+                norm_half(idx, t)
 
             if t == 0:
-                @pl.when(idx > 0)
-                def _():
-                    for u in range(2):
-                        for c in n_copies(idx - 1, u):
-                            c.wait()
-                    send_piece(idx - 1)
-        return 0
-
-    lax.fori_loop(0, n_pieces + 1, norm_step, 0)
+                for u in range(2):
+                    for c in n_copies(idx - 1, u):
+                        c.wait()
+                send_piece(idx - 1)
+        return 0
+
+    for t in range(2):
+        norm_half(0, t)
+    pl.semaphore_wait(barrier, 3)
+    lax.fori_loop(1, n_pieces + 1, norm_step, 0)
 
     def unit_rows(t, emit):
         @pl.when(t < own_units)
@@ -217,7 +222,7 @@
         return 0
 
     def handled(s):
-        return jnp.minimum(n_chunks - nk, jnp.maximum(s - (local_units * nk - 2), 4 + (2 * s) // 3))
+        return jnp.minimum(n_chunks - nk + EARLY, jnp.maximum(s - (local_units * nk - 2), 4 + (2 * s) // 3))
 
     load(0, True)
 
@@ -264,16 +269,16 @@
                         pltpu.make_async_copy(ost.at[p, pl.ds(i * PIECE, PIECE)], outs[p].at[pl.ds(row, PIECE)], out_sem.at[p, i]).start()
             unit_rows(t, emit)
 
+    def partial_step(t, kc, _):
+        s = t * nk + kc
+        before(s)
+        for p in range(3):
+            cols = slice(p * width, (p + 1) * width)
+            acc[:, cols] = jnp.where(kc == 0, 0.0, acc[:, cols]) + product(s, kc, p)
+        return 0
+
     def unit(t, _):
-        def partial_step(kc, _):
-            s = t * nk + kc
-            before(s)
-            for p in range(3):
-                cols = slice(p * width, (p + 1) * width)
-                acc[:, cols] = jnp.where(kc == 0, 0.0, acc[:, cols]) + product(s, kc, p)
-            return 0
-
-        lax.fori_loop(0, nk - 1, partial_step, 0)
+        lax.fori_loop(0, nk - 1, functools.partial(partial_step, t), 0)
         s = t * nk + nk - 1
         before(s)
 
@@ -292,6 +297,10 @@
     lax.fori_loop(0, n_units, unit, 0)
     store(n_units - 1, True)
 
+    lax.fori_loop(0, EARLY, functools.partial(partial_step, n_units), 0)
+    keep = pltpu.make_async_copy(acc, partial, partial_sem)
+    keep.start()
+
     def drain(m, _):
         for d in range(2):
             ici_copy(d, 0, 0, m).wait_send()
@@ -305,15 +314,16 @@
     lax.fori_loop(0, n_pieces, drain_own, 0)
     lax.fori_loop(0, n_chunks - nk, drain, 0)
 
-    lax.fori_loop(n_chunks - nk, n_chunks, handle, 0)
+    lax.fori_loop(n_chunks - nk + EARLY, n_chunks, handle, 0)
     lax.fori_loop(n_chunks - nk, n_chunks, drain, 0)
-    for kc in range(nk):
+    keep.wait()
+    for kc in range(EARLY, nk):
         for d in range(2):
             d2d_copy(d, src_row(d, sib_lane, 2, per_half - 1), kc, n_chunks - nk + kc).wait_recv()
 
 
-def finish_kernel(n, w2, gathered, q_in, k_in, v_in, q_out, k_out, v_out,
-                  xt, acc, st, ost, buf, load_sem, read_sem, write_sem, out_sem):
+def finish_kernel(n, w2, gathered, partial, q_in, k_in, v_in, q_out, k_out, v_out,
+                  xt, acc, st, ost, buf, load_sem, acc_sem, read_sem, write_sem, out_sem):
     ins, outs = (q_in, k_in, v_in), (q_out, k_out, v_out)
     total_rows, dim = gathered.shape
     rows = total_rows // n
@@ -323,9 +333,13 @@
     chips = n // 2
     chip_rows = 2 * rows
     slots, span = buf.shape[0], buf.shape[2]
-
-    far = (lax.axis_index("tp") // 2 + chips // 2) % chips
-    unit_rows = [pl.multiple_of(far * chip_rows + end - PIECE, PIECE) for end in range(half, chip_rows + 1, half)]
+    first = EARLY * KC
+    deep = dim - first
+
+    me = lax.axis_index("tp")
+    lane = me % 2
+    far = (me // 2 + chips // 2) % chips
+    unit_rows = [pl.multiple_of((far * 2 + w) * rows + end - PIECE, PIECE) for w in (lane, 1 - lane) for end in (half, rows)]
     moves = []
     for other in range(1, chips):
         base = ((far + other) % chips) * chip_rows
@@ -350,72 +364,57 @@
         for c in copies:
             c.wait()
 
-    deep = dim // 2
-
-    def loads(k):
-        return [pltpu.make_async_copy(
-            gathered.at[pl.ds(row, PIECE), pl.ds(k * deep, deep)],
-            xt.at[pl.ds(i * PIECE, PIECE), pl.ds(k * deep, deep)], load_sem.at[k, i]) for i, row in enumerate(unit_rows)]
+    n_cols = width // 2
+    n_dots = 3 * width // n_cols
+    heads = n_cols // head
+    loads = [pltpu.make_async_copy(
+        gathered.at[pl.ds(row, PIECE), pl.ds(first, deep)], xt.at[pl.ds(i * PIECE, PIECE)], load_sem.at[i])
+        for i, row in enumerate(unit_rows)]
+    sums = [pltpu.make_async_copy(partial.at[:, pl.ds(i * n_cols, n_cols)], acc.at[:, pl.ds(i * n_cols, n_cols)], acc_sem.at[i])
+            for i in range(n_dots)]
 
     def result(p):
         return [pltpu.make_async_copy(ost.at[p, pl.ds(i * PIECE, PIECE)], outs[p].at[pl.ds(row, PIECE)], out_sem.at[p, i])
                 for i, row in enumerate(unit_rows)]
 
-    n_read, n_written, n_freed = 0, 0, 0
-    for k in range(2):
-        start(loads(k))
-    for _ in range(FIRST_READS):
-        start(read(n_read))
-        n_read += 1
-    wait(loads(0))
-    while n_read < slots:
-        start(read(n_read))
-        n_read += 1
-
-    n_cols = acc.shape[1]
-    n_dots = 2 * (3 * width // n_cols)
-    per_p = width // n_cols
-    heads = n_cols // head
+    start(loads)
+    start(sums[:1])
+    for j in range(FIRST_READS):
+        start(read(j))
+    start(sums[1:])
+    for j in range(FIRST_READS, slots):
+        start(read(j))
+
+    count = {"read": slots, "written": 0, "freed": 0}
+
+    def advance():
+        j = count["written"]
+        wait(read(j))
+        start(write(j))
+        count["written"] += 1
+        if count["written"] - count["freed"] > LAG:
+            wait(write(count["freed"]))
+            count["freed"] += 1
+            if count["read"] < len(moves):
+                start(read(count["read"]))
+                count["read"] += 1
+
+    wait(loads)
     for i_dot in range(n_dots):
-        nb, k = i_dot // 2, i_dot % 2
-        if i_dot == 1:
-            wait(loads(1))
-        part = jnp.dot(xt[:, k * deep:(k + 1) * deep], w2[k * deep:(k + 1) * deep, nb * n_cols:(nb + 1) * n_cols],
-                       preferred_element_type=F32)
-        if k == 0:
-            acc[...] = part
-        else:
-            part = acc[...] + part
-            p = nb // per_p
-            for i in range(heads):
-                st[pl.ds((nb % per_p) * heads + i, UNIT, stride=n_heads), :] = part[:, i * head:(i + 1) * head]
-            if nb % per_p == per_p - 1:
-                ost[p] = st[...].reshape(UNIT, n_heads, head).astype(BF16)
-                start(result(p))
-        free = n_written
-        target = min(len(moves), -(-len(moves) * (i_dot + 1) // (n_dots - 1)))
-        while n_written < min(target, n_read):
-            wait(read(n_written))
-            start(write(n_written))
-            n_written += 1
-        while n_freed < free:
-            wait(write(n_freed))
-            n_freed += 1
-            if n_read < len(moves):
-                start(read(n_read))
-                n_read += 1
-    while n_written < len(moves):
-        while n_freed < n_written and n_read < len(moves):
-            wait(write(n_freed))
-            n_freed += 1
-            start(read(n_read))
-            n_read += 1
-        wait(read(n_written))
-        start(write(n_written))
-        n_written += 1
-    while n_freed < len(moves):
-        wait(write(n_freed))
-        n_freed += 1
+        p, cols = i_dot // 2, slice(i_dot * n_cols, (i_dot + 1) * n_cols)
+        wait(sums[i_dot:i_dot + 1])
+        part = acc[:, cols] + jnp.dot(xt[...], w2[first:, cols], preferred_element_type=F32)
+        for i in range(heads):
+            st[pl.ds((i_dot % 2) * heads + i, UNIT, stride=n_heads), :] = part[:, i * head:(i + 1) * head]
+        if i_dot % 2 == 1:
+            ost[p] = st[...].reshape(UNIT, n_heads, head).astype(BF16)
+            start(result(p))
+        for _ in range(3):
+            advance()
+    while count["written"] < len(moves):
+        advance()
+    for j in range(count["freed"], len(moves)):
+        wait(write(j))
     for p in range(3):
         wait(result(p))
 
@@ -433,11 +432,12 @@
         hbm = pl.BlockSpec(memory_space=pl.ANY)
         vmem = pl.BlockSpec(memory_space=pltpu.VMEM)
         room = 67043328 - 2 * dim * 3 * width
-        q, k, v, gathered, w2 = pl.pallas_call(
+        q, k, v, gathered, w2, partial = pl.pallas_call(
             functools.partial(fused_kernel, n),
-            out_shape=(out, out, out, jax.ShapeDtypeStruct((n * rows, dim), BF16), pltpu.VMEM((dim, 3 * width), BF16)),
+            out_shape=(out, out, out, jax.ShapeDtypeStruct((n * rows, dim), BF16), pltpu.VMEM((dim, 3 * width), BF16),
+                       jax.ShapeDtypeStruct((UNIT, 3 * width), F32)),
             in_specs=[hbm, vmem, hbm, hbm, hbm],
-            out_specs=(hbm, hbm, hbm, hbm, vmem),
+            out_specs=(hbm, hbm, hbm, hbm, vmem, hbm),
             scratch_shapes=[
                 pltpu.VMEM((UNIT, 3 * width), F32),
                 pltpu.VMEM((2, UNIT, KC), BF16),
@@ -445,7 +445,7 @@
                 pltpu.VMEM((3, UNIT, n_heads, head), BF16),
                 pltpu.VMEM((3, WB, n_heads, head), BF16),
                 pltpu.VMEM((4, SUB, dim), BF16),
-                dma((4,)), dma((4, dim // KC)), dma((2, 3)), dma((2, 4)), dma((3, 4)),
+                dma((4,)), dma((4, dim // KC)), dma((2, 3)), dma((2, 4)), dma((3, 4)), dma,
                 dma((rows // PIECE,)), dma((rows // PIECE,)),
                 dma((2, chunks)), dma((2, chunks)), dma((2, chunks)), dma((2, chunks)),
             ],
@@ -456,19 +456,19 @@
         return pl.pallas_call(
             functools.partial(finish_kernel, n),
             out_shape=(out, out, out),
-            in_specs=[vmem, hbm, hbm, hbm, hbm],
+            in_specs=[vmem, hbm, hbm, hbm, hbm, hbm],
             out_specs=(hbm, hbm, hbm),
             scratch_shapes=[
-                pltpu.VMEM((UNIT, dim), BF16),
-                pltpu.VMEM((UNIT, width // 2), F32),
+                pltpu.VMEM((UNIT, dim - EARLY * KC), BF16),
+                pltpu.VMEM((UNIT, 3 * width), F32),
                 pltpu.VMEM((UNIT * n_heads, head), F32),
                 pltpu.VMEM((3, UNIT, n_heads, head), BF16),
                 pltpu.VMEM((SLOTS, 3, SPAN, n_heads, head), BF16),
-                dma((2, 4)), dma((SLOTS, 3)), dma((SLOTS, 3)), dma((3, 4)),
+                dma((4,)), dma((6,)), dma((SLOTS, 3)), dma((SLOTS, 3)), dma((3, 4)),
             ],
             compiler_params=pltpu.CompilerParams(vmem_limit_bytes=room),
             name="finish",
-        )(pltpu.with_memory_space_constraint(w2, pltpu.VMEM), gathered, q, k, v)
+        )(pltpu.with_memory_space_constraint(w2, pltpu.VMEM), gathered, partial, q, k, v)
 
     row_spec = P(("dp", "tp"), None)
     head_spec = P(None, "tp", None)

time: 305 us -> 313 us (1.026)
  Pallas kernels: 304 us -> 312 us
    pallas_call x1, Pallas kernels: 284 us -> 290 us  [local_step(): pl.pallas_call(functools.partial(fused_kernel, n), out_shape=(out, out, o...]
where the time goes in v4:
time: 313 us
  Pallas kernels  312 us (100%)
    pallas_call x1, Pallas kernels, local_step(): pl.pallas_call(functools.partial(fused_kernel, n), out_shape=(out, out, o...  290 us
    pallas_call x1, Pallas kernels, local_step(): pl.pallas_call(functools.partial(finish_kernel, n), out_shape=(out, out,...  21.6 us

profile of v4, /device:TPU:81, one launch (start us, length us, event | category | flops | bytes accessed | tf_op | source)
XLA Modules:
  0.0 312.5 jit_solution(10609832682375703025)
XLA Ops:
  0.6 290.1 %norm_gather_project.1 = (bf16[4096,8,128]{2,1,0:T(8,128)(2,1)}, bf16[4096,8,128]{2,1,0:T(8,128)(2,1)}, bf16[4096,8,128]{2,1,0:T(8,128)(2,1)}, bf16[4096,8192]{1...) custom-call(bf16[512,8192]{1,0:T(8,128)(2,1)} %x_hbm.1, f32[1,8192]{1,0:T(1,128)} %bitcast.1, ...), custom_call_target="tpu_custom_call" | custom-call | tf_op jit(solution)/shard_map/norm_gather_project/pallas_call | solution.py:435
  290.7 21.6 %finish.1 = (bf16[4096,8,128]{2,1,0:T(8,128)(2,1)}, bf16[4096,8,128]{2,1,0:T(8,128)(2,1)}, bf16[4096,8,128]{2,1,0:T(8,128)(2,1)}) custom-call(bf16[8192,3072]{1,0:T(8,128)(2,1)S(1)} %get-tuple-element.9.w2, bf16[4096,8192]{1,0:T(8,128)(2,1)} %get-tuple-element.10.gathered, f32[256,3072]{1,0:T(8,128)} %get-tuple-element.11.partial, ...), custom_call_target="tpu_custom_call" | custom-call | tf_op jit(solution)/shard_map/finish/pallas_call | solution.py:456
